TPU v7x, 32 devices: a whole 2x2x4 slice. The times are simulated.
32 devices in a mesh: row: 8 (over z, x), col: 4 (over y, core).
Axes of the slice: x: 2, y: 2, z: 4, core: 2. Of those that a mesh axis runs over, the one named last changes fastest.
Arguments:
- old_params: float32 [2, 64, 131072], P(None, ('row', 'col')), may hold values from -0.12 to 0.12
- old_first: float32 [2, 64, 131072], P(None, ('row', 'col')), may hold values from -1.8 to 1.8
- old_second: float32 [2, 64, 131072], P(None, ('row', 'col')), may hold values from 0.001 to 1
- gradients: float32 [2, 32, 262144], P(None, ('row', 'col')), may hold values from -250 to 250
- old_table: int32 [2, 64], replicated, may hold values from 0 to 63, as said below
- new_table: int32 [2, 32], replicated, may hold values from 0 to 31, as said below
Outputs:
- new_params: float32 [2, 32, 262144], P(None, ('row', 'col'))
- new_first: float32 [2, 32, 262144], P(None, ('row', 'col'))
- new_second: float32 [2, 32, 262144], P(None, ('row', 'col'))
Inputs may be any that keep to these rules, and one draw needn't show every extreme that they name: old_table[t, p] = p XOR k for one k per tensor. new_table[t, q] = q XOR k for one k per tensor.
All inputs are finite; a program needn't handle non-finite values.
Results may differ from a plain program's by a relative error of at most 0.00002.
Values sent between devices are 32-bit elements; how exact they have to be, the bound alone decides.
A program may use at most 64 MiB of HBM per device.

v0:
```python
import functools
import math

import jax
import jax.numpy as jnp
from jax import lax
from jax.experimental import pallas as pl
from jax.experimental.pallas import tpu as pltpu
from jax.sharding import PartitionSpec as P

STEP = 100
LANES = 128
AXES = ("row", "col")
JOINT_DEVICES = 32
GROUPS = 8
SPLIT = 2
PART = 256
BLOCK = 64
SUM_ROWS = 256
LOGICAL = pl.DeviceIdType.LOGICAL


beta_one = 0.9
beta_two = 0.95
epsilon = 1e-08
learn_rate = 0.001
decay_rate = 0.1


def adam_update(params, first_moment, second_moment, gradients, clip_factor):
    scaled = clip_factor * gradients
    first_new = beta_one * first_moment + (1.0 - beta_one) * scaled
    second_new = beta_two * second_moment + (1.0 - beta_two) * scaled * scaled
    rate = learn_rate / (1.0 - beta_one**STEP)
    unbias = 1.0 / (1.0 - beta_two**STEP)
    update = first_new * rate / (jnp.sqrt(second_new * unbias) + epsilon)
    params_new = params * (1.0 - learn_rate * decay_rate) - update
    return (params_new, first_new, second_new)


def partner(key):
    return jnp.bitwise_xor(lax.axis_index(AXES), key)


def clip_kernel(devices, limit, grad_ref, clip_ref, grads, parts, load_sems, sent_sem, landed_sem):
    step = grads.shape[1]
    loads = [
        pltpu.make_async_copy(grad_ref.at[pl.ds(number * step, step)], grads.at[number], load_sems.at[number])
        for number in range(grads.shape[0])
    ]
    for load in loads:
        load.start()
    barrier = pltpu.get_barrier_semaphore()

    def greet(step, _):
        pl.semaphore_signal(barrier, inc=1, device_id=partner(devices - step), device_id_type=LOGICAL)
        return 0

    lax.fori_loop(1, devices, greet, 0)
    rows = min(step, SUM_ROWS)
    squares = jnp.zeros((8, LANES), jnp.float32)
    for number, load in enumerate(loads):
        load.wait()

        def add(line, total, number=number):
            block = grads[number, pl.ds(pl.multiple_of(line * rows, rows), rows)]
            return total + jnp.sum((block * block).reshape(-1, 8, LANES), axis=0)

        squares = lax.fori_loop(0, step // rows, add, squares)
    parts[0] = jnp.sum(squares, axis=0, keepdims=True)
    pl.semaphore_wait(barrier, devices - 1)

    def send(step, _):
        key = devices - step
        pltpu.make_async_remote_copy(
            src_ref=parts.at[0],
            dst_ref=parts.at[key],
            send_sem=sent_sem,
            recv_sem=landed_sem,
            device_id=partner(key),
            device_id_type=LOGICAL,
        ).start()
        return 0

    lax.fori_loop(1, devices, send, 0)
    others = parts.at[pl.ds(1, devices - 1)]
    pltpu.make_async_copy(others, others, landed_sem).wait()
    pltpu.make_async_copy(others, others, sent_sem).wait()
    total = jnp.sum(jnp.sum(parts[...], axis=0), axis=1, keepdims=True)
    clip_ref[...] = jnp.broadcast_to(limit / jnp.maximum(jnp.sqrt(total), limit), clip_ref.shape)


def clip_of(gradients, devices, number):
    limit = 0.5 * math.sqrt(gradients.size * devices)
    loads = 2
    step = gradients.size // LANES // loads
    return pl.pallas_call(
        functools.partial(clip_kernel, devices, limit),
        in_specs=[pl.BlockSpec(memory_space=pl.ANY)],
        out_specs=pl.BlockSpec(memory_space=pltpu.VMEM),
        out_shape=jax.ShapeDtypeStruct((1, LANES), jnp.float32),
        scratch_shapes=[
            pltpu.VMEM((loads, step, LANES), jnp.float32),
            pltpu.VMEM((devices, 1, LANES), jnp.float32),
            pltpu.SemaphoreType.DMA((loads,)),
            pltpu.SemaphoreType.DMA,
            pltpu.SemaphoreType.DMA,
        ],
        compiler_params=pltpu.CompilerParams(collective_id=number, has_side_effects=True),
        name="clip",
    )(gradients.reshape(-1, LANES))


def move_kernel(jobs, params_ref, first_ref, second_ref, out_ref, landed_sems, sent_sem, passed_sem):
    states = (params_ref, first_ref, second_ref)
    moves = [(slot, tensor, key) for slot, (tensor, key) in enumerate(jobs) if key]
    stays = [(slot, tensor) for slot, (tensor, key) in enumerate(jobs) if not key]
    peers = sorted({1} | {key for _, _, key in moves})
    places = {key: partner(key) for key in peers}
    barrier = pltpu.get_barrier_semaphore()
    for place in places.values():
        pl.semaphore_signal(barrier, inc=1, device_id=place, device_id_type=LOGICAL)
    pl.semaphore_wait(barrier, len(peers))
    (groups,) = landed_sems.shape
    halves = params_ref.shape[2]
    group_rows = params_ref.shape[1] // groups
    rows = max(group_rows // SPLIT, 1)
    split = group_rows // rows

    def span(start, size):
        return pl.ds(pl.multiple_of(start * size, size), size)

    def turn(step):
        (slot, tensor, key), (_, _, other) = moves[0], moves[-1]
        if len(moves) == 1:
            return slot, tensor, places[key], step
        bit = jnp.bitwise_and(step, 1)
        place = places[key]
        if key != other:
            place = jnp.where(bit == 0, place, places[other])
        return bit, bit, place, jnp.right_shift(step, 1)

    def window(slot, tensor, piece):
        half, chunk = jnp.bitwise_and(piece, 1), jnp.right_shift(piece, 1)
        for number, state in enumerate(states):
            source = state.at[tensor, span(chunk, rows), half, 0]
            yield source, out_ref.at[0, slot, number, half, span(chunk, rows)], landed_sems.at[lax.div(chunk, split)]

    def start(step, _):
        slot, tensor, place, piece = turn(step)
        for source, target, landed_sem in window(slot, tensor, piece):
            pltpu.make_async_remote_copy(
                src_ref=source,
                dst_ref=target,
                send_sem=sent_sem,
                recv_sem=landed_sem,
                device_id=place,
                device_id_type=LOGICAL,
            ).start()
        return 0

    def keep(step, _):
        slot, tensor, piece = stays[0] + (step,)
        if len(stays) == 2:
            slot, piece = jnp.bitwise_and(step, 1), jnp.right_shift(step, 1)
            tensor = slot
        for source, target, landed_sem in window(slot, tensor, piece):
            pltpu.make_async_copy(source, target, landed_sem).start()
        return 0

    def relay(group, _):
        landed = out_ref.at[0, :, :, :, span(group, group_rows)]
        pltpu.make_async_copy(landed, landed, landed_sems.at[group]).wait()
        pltpu.make_async_remote_copy(
            src_ref=landed,
            dst_ref=out_ref.at[1, :, :, :, span(group, group_rows)],
            send_sem=sent_sem,
            recv_sem=passed_sem,
            device_id=places[1],
            device_id_type=LOGICAL,
        ).start()
        return 0

    pieces = groups * split * halves
    if moves:
        lax.fori_loop(0, pieces * len(moves), start, 0)
    if stays:
        lax.fori_loop(0, pieces * len(stays), keep, 0)
    lax.fori_loop(0, groups, relay, 0)
    passed = out_ref.at[1]
    sent = passed if stays else out_ref
    pltpu.make_async_copy(sent, sent, sent_sem).wait()
    if moves and stays:
        moved = out_ref.at[0, moves[0][0]]
        pltpu.make_async_copy(moved, moved, sent_sem).wait()
    pltpu.make_async_copy(passed, passed, passed_sem).wait()


def move(jobs, number, arrays):
    _, rows, halves, _, lanes = arrays[0].shape
    groups = min(GROUPS, rows)
    return pl.pallas_call(
        functools.partial(move_kernel, jobs),
        in_specs=[pl.BlockSpec(memory_space=pl.ANY)] * 3,
        out_specs=pl.BlockSpec(memory_space=pl.ANY),
        out_shape=jax.ShapeDtypeStruct((2, len(jobs), 3, halves, rows, lanes), jnp.float32),
        scratch_shapes=[pltpu.SemaphoreType.DMA((groups,))] + [pltpu.SemaphoreType.DMA] * 2,
        compiler_params=pltpu.CompilerParams(
            collective_id=number, has_side_effects=True, vmem_limit_bytes=1 << 20
        ),
        name="move_" + "_".join(str(key) for _, key in jobs),
    )(*arrays)


def update_kernel(table_ref, clip_ref, moved_ref, grad_ref, params_out, first_out, second_out, *scratch):
    moved, results, moved_sems, out_sems = scratch
    parts, _, rows, _ = moved.shape
    halves = grad_ref.shape[1]
    blocks = grad_ref.shape[2] // rows
    block_rows = min(rows, BLOCK)
    outs = (params_out, first_out, second_out)
    clip_factor = clip_ref[...]

    def place(part):
        block, shard = lax.rem(part, blocks), lax.div(part, blocks)
        return lax.div(shard, halves), lax.rem(shard, halves), pl.ds(pl.multiple_of(block * rows, rows), rows)

    def load(part):
        tensor, half, span = place(part)
        source = moved_ref.at[table_ref[0, tensor], tensor, :, jnp.bitwise_xor(half, table_ref[1, tensor]), span]
        return pltpu.make_async_copy(source, moved.at[part], moved_sems.at[part])

    def stores(part):
        tensor, half, span = place(part)
        return [
            pltpu.make_async_copy(results.at[part, number], out.at[tensor, half, span], out_sems.at[number, part])
            for number, out in enumerate(outs)
        ]

    def begin(part, _):
        load(part).start()
        return 0

    def compute(part, _):
        load(part).wait()
        tensor, half, whole = place(part)

        def block(number, _):
            span = pl.ds(pl.multiple_of(number * block_rows, block_rows), block_rows)
            grads = grad_ref[tensor, half, pl.ds(pl.multiple_of(whole.start + number * block_rows, block_rows), block_rows)]
            values = adam_update(moved[part, 0, span], moved[part, 1, span], moved[part, 2, span], grads, clip_factor)
            for number, value in enumerate(values):
                results[part, number, span] = value
            return 0

        lax.fori_loop(0, rows // block_rows, block, 0)
        for copy in stores(part):
            copy.start()
        return 0

    def finish(part, _):
        for copy in stores(part):
            copy.wait()
        return 0

    lax.fori_loop(0, parts, begin, 0)
    lax.fori_loop(0, parts, compute, 0)
    lax.fori_loop(0, parts, finish, 0)


def update(table, clip_factor, moved, gradients):
    tensors, halves, rows, lanes = gradients.shape
    step = min(rows, PART)
    parts = tensors * halves * (rows // step)
    return pl.pallas_call(
        update_kernel,
        in_specs=[
            pl.BlockSpec(memory_space=pltpu.SMEM),
            pl.BlockSpec(memory_space=pltpu.VMEM),
            pl.BlockSpec(memory_space=pl.ANY),
            pl.BlockSpec(memory_space=pltpu.VMEM),
        ],
        out_specs=[pl.BlockSpec(memory_space=pl.ANY)] * 3,
        out_shape=[jax.ShapeDtypeStruct(gradients.shape, jnp.float32)] * 3,
        scratch_shapes=[
            pltpu.VMEM((parts, 3, step, lanes), jnp.float32),
            pltpu.VMEM((parts, 3, step, lanes), jnp.float32),
            pltpu.SemaphoreType.DMA((parts,)),
            pltpu.SemaphoreType.DMA((3, parts)),
        ],
        compiler_params=pltpu.CompilerParams(vmem_limit_bytes=20 << 20),
        name="update",
    )(table, clip_factor, moved, gradients)


def shards(old_params, old_first, old_second, gradients, old_table, new_table):
    tensors, halves, width = old_params.shape
    devices = lax.axis_size(AXES)
    rows = width // LANES
    old_key = old_table[:, 0]
    keys = jnp.bitwise_xor(jnp.right_shift(old_key, 1), new_table[:, 0])
    table = jnp.stack([jnp.bitwise_and(keys, 1), jnp.bitwise_and(old_key, 1)])
    chip_keys = jnp.right_shift(keys, 1)

    def paired(array):
        return array.reshape(tensors, halves, rows, 1, LANES).transpose(0, 2, 1, 3, 4)

    flat = gradients.reshape(tensors, halves, rows, LANES)
    clip_factor = clip_of(gradients, devices, 0)
    chip_keys, clip_factor = lax.optimization_barrier((chip_keys, clip_factor))
    chips = devices // 2
    states = (paired(old_params), paired(old_first), paired(old_second))
    if devices <= JOINT_DEVICES:

        def inner(one, arrays):
            branches = [
                functools.partial(move, ((0, 2 * one), (1, 2 * two)), 1 + one * chips + two) for two in range(chips)
            ]
            return lax.switch(chip_keys[1], branches, arrays)

        moved = lax.switch(chip_keys[0], [functools.partial(inner, one) for one in range(chips)], states)
    else:
        moved = []
        for tensor in range(tensors):
            branches = [
                functools.partial(move, ((tensor, 2 * i),), 1 + tensor * chips + i) for i in range(chips)
            ]
            moved.append(lax.switch(chip_keys[tensor], branches, states))
        moved = jnp.concatenate(moved, axis=1)
    results = update(table, clip_factor, moved, flat)
    return tuple(result.reshape(gradients.shape) for result in results)


def solution(mesh):
    spec = P(None, AXES, None)
    return jax.shard_map(
        shards,
        mesh=mesh,
        in_specs=(spec, spec, spec, spec, P(), P()),
        out_specs=(spec, spec, spec),
        check_vma=False,
    )
```

profile of v0, /device:TPU:9, one launch (start us, length us, event | category | flops | bytes accessed | tf_op | source)
XLA Modules:
  0.0 166.7 jit_solution(1180914824169968525)
XLA Ops:
  0.6 8.8 %clip.1.clip_ref = f32[1,128]{1,0:T(1,128)} custom-call(f32[4096,128]{1,0:T(8,128)} %bitcast.34), custom_call_target="tpu_custom_call" | custom-call | tf_op jit(solution)/shard_map/clip/pallas_call | solution.py:97
  9.4 0.8 shift-right-arithmetic_reduce_fusion
  10.3 0.0 copy-start
  10.3 0.0 copy-start.1
  10.3 149.6 %conditional.17 = (f32[2,2,3,2,1024,128]{5,4,3,2,1,0:T(8,128)}) conditional(s32[]{:T(128)} %bitcast.17, (s32[2]{0:T(128)S(1)}, f32[2,1024,2,1,128]{4,3,2,1,0:T(1,128)}, f32[2,1024,2,1,128]{4,3,2,1,0:T(1,128)}, f32[2,1024,2,1,128]{4,3,2,1,0:T(1,128)}) %tuple.1135, (s32[2]{0:T(128)S(1)}, ...), branch_computations={%region_0.0_spmd, %region_17.0_spmd, %region_34.0_spmd, %region_51... | conditional | flops 1 | bytes 56 | solution.py:321
  10.4 0.6 slice.40
  11.6 147.8 %conditional.2 = (f32[2,2,3,2,1024,128]{5,4,3,2,1,0:T(8,128)}) conditional(s32[]{:T(128)} %bitcast.2, (f32[2,1024,2,1,128]{4,3,2,1,0:T(1,128)}, f32[2,1024,2,1,128]{4,3,2,1,0:T(1,128)}, f32[2,1024,2,1,128]{4,3,2,1,0:T(1,128)}) %tuple.582, (f32[2,1024,2,1,128]{4,3,2,1,0:T(1,128)}, f32[2,1024,2,1,128]{4,3,2,1,0:T(1,128)}, ...), branch_computations={%region_35.0_spmd, %region_36.0_spmd, %region_37.0_spmd, %region_3... | conditional | bytes 8 | solution.py:319
  11.6 147.7 %move_4_26.1 = f32[2,2,3,2,1024,128]{5,4,3,2,1,0:T(8,128)} custom-call(f32[2,1024,2,1,128]{4,3,2,1,0:T(1,128)} %get-tuple-element.1978.params_ref, f32[2,1024,2,1,128]{4,3,2,1,0:T(1,128)} %get-tuple-element.1979.first_ref, f32[2,1024,2,1,128]{4,3,2,1,0:T(1,128)} %get-tuple-element.1984.second_ref), custom_call_target="tpu_custom_call" | custom-call | tf_op jit(solution)/shard_map/cond/branch_2_fun/cond/branch_13_fun/move_4_26/pallas_call | solution.py:202
  160.0 0.0 copy-done
  160.0 0.0 copy-done.1
  160.0 6.5 %update.1 = (f32[2,2,1024,128]{3,2,1,0:T(8,128)}, f32[2,2,1024,128]{3,2,1,0:T(8,128)}, f32[2,2,1024,128]{3,2,1,0:T(8,128)}) custom-call(s32[2,2]{1,0:T(2,128)S(1)} %pad_add_fusion.table_ref, f32[1,128]{1,0:T(1,128)S(1)} %copy-done.1, f32[2,2,3,2,1024,128]{5,4,3,2,1,0:T(8,128)} %get-tuple-element.2820.moved_ref, f32[2,2,1024,128]{3,2,1,0:T(8,128)S(1)} %bitcast.35), custom_call_target="tpu_custom_call" | custom-call | tf_op jit(solution)/shard_map/update/pallas_call | solution.py:275
  (1 shorter events, 0.0 us)
Async XLA Ops:
  10.3 149.7 %copy-start = (f32[2,1,262144]{2,1,0:T(1,128)S(1)}, f32[2,1,262144]{2,1,0:T(1,128)}, u32[]{:S(2)}) copy-start(f32[2,1,262144]{2,1,0:T(1,128)} %param.281) | copy-start | bytes 6291460
  10.3 149.6 %copy-start.1 = (f32[1,128]{1,0:T(1,128)S(1)}, f32[1,128]{1,0:T(1,128)}, u32[]{:S(2)}) copy-start(f32[1,128]{1,0:T(1,128)} %clip.1.clip_ref) | copy-start | bytes 1540
where the time goes:
time: 167 us
  Pallas kernels  163 us (98%)
    pallas_call x1, Pallas kernels, move(): pl.pallas_call(functools.partial(move_kernel, jobs), in_specs=[pl.BlockSp...  148 us
    pallas_call x1, Pallas kernels, clip_of(): pl.pallas_call(functools.partial(clip_kernel, devices, limit), in_specs=[...  8.76 us
    pallas_call x1, Pallas kernels, update(): pl.pallas_call(update_kernel, in_specs=[pl.BlockSpec(memory_space=pltpu.S...  6.54 us

commit v1 on v0

--- a/solution.py
+++ b/solution.py
@@ -14,8 +14,8 @@
 JOINT_DEVICES = 32
 GROUPS = 8
 SPLIT = 2
-PART = 256
-BLOCK = 64
+PART = 1024
+BLOCK = 256
 SUM_ROWS = 256
 LOGICAL = pl.DeviceIdType.LOGICAL
 

time: 167 us -> 166 us (level)
  Pallas kernels: 163 us -> 161 us
where the time goes in v1:
time: 166 us; the launch traced here: 165 us
  Pallas kernels  161 us (97%)
    pallas_call x1, Pallas kernels, move(): pl.pallas_call(functools.partial(move_kernel, jobs), in_specs=[pl.BlockSp...  147 us
    pallas_call x1, Pallas kernels, clip_of(): pl.pallas_call(functools.partial(clip_kernel, devices, limit), in_specs=[...  8.76 us
    pallas_call x1, Pallas kernels, update(): pl.pallas_call(update_kernel, in_specs=[pl.BlockSpec(memory_space=pltpu.S...  5.2 us

profile of v1, /device:TPU:9, one launch (start us, length us, event | category | flops | bytes accessed | tf_op | source)
XLA Modules:
  0.0 165.2 jit_solution(10845511760317730014)
XLA Ops:
  0.6 8.8 %clip.1.clip_ref = f32[1,128]{1,0:T(1,128)} custom-call(f32[4096,128]{1,0:T(8,128)} %bitcast.34), custom_call_target="tpu_custom_call" | custom-call | tf_op jit(solution)/shard_map/clip/pallas_call | solution.py:97
  9.4 0.8 shift-right-arithmetic_reduce_fusion
  10.3 0.0 copy-start
  10.3 0.0 copy-start.1
  10.3 149.5 %conditional.17 = (f32[2,2,3,2,1024,128]{5,4,3,2,1,0:T(8,128)}) conditional(s32[]{:T(128)} %bitcast.17, (s32[2]{0:T(128)S(1)}, f32[2,1024,2,1,128]{4,3,2,1,0:T(1,128)}, f32[2,1024,2,1,128]{4,3,2,1,0:T(1,128)}, f32[2,1024,2,1,128]{4,3,2,1,0:T(1,128)}) %tuple.1135, (s32[2]{0:T(128)S(1)}, ...), branch_computations={%region_0.0_spmd, %region_17.0_spmd, %region_34.0_spmd, %region_51... | conditional | flops 1 | bytes 56 | solution.py:321
  10.4 0.6 slice.42
  11.6 147.5 %conditional.4 = (f32[2,2,3,2,1024,128]{5,4,3,2,1,0:T(8,128)}) conditional(s32[]{:T(128)} %bitcast.4, (f32[2,1024,2,1,128]{4,3,2,1,0:T(1,128)}, f32[2,1024,2,1,128]{4,3,2,1,0:T(1,128)}, f32[2,1024,2,1,128]{4,3,2,1,0:T(1,128)}) %tuple.614, (f32[2,1024,2,1,128]{4,3,2,1,0:T(1,128)}, f32[2,1024,2,1,128]{4,3,2,1,0:T(1,128)}, ...), branch_computations={%region_69.0_spmd, %region_70.0_spmd, %region_71.0_spmd, %region_7... | conditional | bytes 8 | solution.py:319
  11.6 147.4 %move_8_28.1 = f32[2,2,3,2,1024,128]{5,4,3,2,1,0:T(8,128)} custom-call(f32[2,1024,2,1,128]{4,3,2,1,0:T(1,128)} %get-tuple-element.2194.params_ref, f32[2,1024,2,1,128]{4,3,2,1,0:T(1,128)} %get-tuple-element.2195.first_ref, f32[2,1024,2,1,128]{4,3,2,1,0:T(1,128)} %get-tuple-element.2196.second_ref), custom_call_target="tpu_custom_call" | custom-call | tf_op jit(solution)/shard_map/cond/branch_4_fun/cond/branch_14_fun/move_8_28/pallas_call | solution.py:202
  159.8 0.0 copy-done
  159.8 0.0 copy-done.1
  159.8 5.2 %update.1 = (f32[2,2,1024,128]{3,2,1,0:T(8,128)}, f32[2,2,1024,128]{3,2,1,0:T(8,128)}, f32[2,2,1024,128]{3,2,1,0:T(8,128)}) custom-call(s32[2,2]{1,0:T(2,128)S(1)} %pad_add_fusion.table_ref, f32[1,128]{1,0:T(1,128)S(1)} %copy-done.1, f32[2,2,3,2,1024,128]{5,4,3,2,1,0:T(8,128)} %get-tuple-element.2820.moved_ref, f32[2,2,1024,128]{3,2,1,0:T(8,128)S(1)} %bitcast.35), custom_call_target="tpu_custom_call" | custom-call | tf_op jit(solution)/shard_map/update/pallas_call | solution.py:275
  (1 shorter events, 0.0 us)
Async XLA Ops:
  10.3 149.5 %copy-start = (f32[2,1,262144]{2,1,0:T(1,128)S(1)}, f32[2,1,262144]{2,1,0:T(1,128)}, u32[]{:S(2)}) copy-start(f32[2,1,262144]{2,1,0:T(1,128)} %param.281) | copy-start | bytes 6291460
  10.3 149.5 %copy-start.1 = (f32[1,128]{1,0:T(1,128)S(1)}, f32[1,128]{1,0:T(1,128)}, u32[]{:S(2)}) copy-start(f32[1,128]{1,0:T(1,128)} %clip.1.clip_ref) | copy-start | bytes 1540
